TPU v7x, 32 devices: a whole 2x2x4 slice. The times are simulated.
32 devices in a mesh: seq: 4 (over z), head: 8 (over y, x, core).
Axes of the slice: x: 2, y: 2, z: 4, core: 2. Of those that a mesh axis runs over, the one named last changes fastest.
Arguments:
- query: bfloat16 [8192, 1024], P('seq', 'head'), may hold values from -15 to 15
- key: bfloat16 [8192, 1024], P('seq', 'head'), may hold values from -6 to 6
- value: bfloat16 [8192, 1024], P('seq', 'head'), may hold values from -50 to 50
- grad_out: bfloat16 [8192, 1024], P('seq', 'head'), may hold values from -6 to 6
- log_decay: float32 [8, 8192], P('head', 'seq'), may hold values from -2.5 to 0
- gain: float32 [1024], P('head'), may hold values from 0.25 to 1.75
Outputs:
- grad_query: bfloat16 [8192, 1024], P('seq', 'head')
- grad_key: bfloat16 [8192, 1024], P('seq', 'head')
- grad_value: bfloat16 [8192, 1024], P('seq', 'head')
All inputs are finite; a program needn't handle non-finite values.
Results may differ from a plain program's by a relative error of at most 0.0063.
Values sent between devices are 32-bit elements; how exact they have to be, the bound alone decides.
A program may use at most 64 MiB of HBM per device.

v0:
```python
import functools

import jax
import jax.numpy as jnp
from jax import lax
from jax.experimental import pallas as pl
from jax.experimental.pallas import tpu as pltpu
from jax.sharding import PartitionSpec as P

BLK = 512
TILE = 256
EPS = 1e-06
F32 = jnp.float32
BF16 = jnp.bfloat16
MESH = pl.DeviceIdType.MESH


def dot(a, b, ca=1, cb=0):
    return lax.dot_general(a, b, (((ca,), (cb,)), ((), ())), preferred_element_type=F32)


def flip(x):
    n = x.shape[1]
    eye = lax.broadcasted_iota(jnp.int32, (n, n), 0) == lax.broadcasted_iota(jnp.int32, (n, n), 1)
    return dot(jnp.where(eye, 1.0, 0.0).astype(BF16), x, 1, 1)


def lanes(x, width):
    return jnp.concatenate([x] * (width // x.shape[1]), axis=1)


def kernel(
    n_seq, n_head, features,
    q_hbm, k_hbm, v_hbm, y_hbm, decay_ref, gain_ref,
    gq_hbm, gk_hbm, gv_hbm,
    q_ref, k_ref, v_ref, y_ref, kt_ref, qt_ref, vt_ref, queried_ref, scaled_ref,
    c_ref, a_ref, col_ref, inner_ref, mix_ref, out_ref, dout_ref,
    state_ref, rear_ref, held_ref, gk_ref, gv_ref, oq_ref, ok_ref, ov_ref, edge_ref,
    tx_ref, rx_ref, stat_ref, stats_ref,
    in_sem, out_sem, send_sem, recv_sem, hsend_sem, hrecv_sem,
):
    seq = lax.axis_index("seq")
    head = lax.axis_index("head")
    tokens, width = q_ref.shape
    nblk = tokens // BLK
    tiles = BLK // TILE

    loads = [
        pltpu.make_async_copy(src, dst, in_sem.at[i])
        for i, (src, dst) in enumerate(
            ((k_hbm, k_ref), (v_hbm, v_ref), (q_hbm, q_ref), (y_hbm, y_ref))
        )
    ]
    for load in loads:
        load.start()

    barrier = pltpu.get_barrier_semaphore()
    for d in range(1, n_seq):
        pl.semaphore_signal(
            barrier, inc=1, device_id={"seq": lax.rem(seq + d, n_seq)}, device_id_type=MESH
        )
    for d in range(1, n_head):
        pl.semaphore_signal(
            barrier, inc=1, device_id={"head": lax.rem(head + d, n_head)}, device_id_type=MESH
        )

    def span(b, start=0, size=BLK):
        return pl.ds(b * BLK + start, size)

    rows = c_ref.shape[0]
    x = jnp.concatenate(
        [decay_ref[:, b * BLK:(b + 1) * BLK] for b in range(nblk)]
        + ([jnp.zeros((rows - nblk, BLK), F32)] if rows > nblk else []),
        axis=0,
    )
    x1 = x.astype(BF16).astype(F32)
    x2 = (x - x1).astype(BF16).astype(F32)
    x3 = x - x1 - x2
    parts = jnp.concatenate([x1, x2, x3, jnp.zeros_like(x)], axis=0).astype(BF16)
    upper = jnp.where(
        lax.broadcasted_iota(jnp.int32, (BLK, BLK), 0)
        <= lax.broadcasted_iota(jnp.int32, (BLK, BLK), 1),
        1.0, 0.0,
    ).astype(BF16)
    sums = dot(parts, upper)
    c_all = sums[:rows] + sums[rows:2 * rows] + sums[2 * rows:3 * rows]
    c_ref[...] = c_all
    a_ref[...] = jnp.broadcast_to(c_all[:, BLK - 1:BLK], (rows, width))

    def c_row(b):
        return c_ref[b:b + 1, :]

    def a_row(b):
        return a_ref[b:b + 1, :]

    loads[0].wait()
    loads[1].wait()
    state = jnp.zeros((width, width), F32)
    own = jnp.zeros((1, width), F32)
    for b in range(nblk):
        state_ref[b] = state
        kt = flip(k_ref[span(b), :])
        kt_ref[:, span(b)] = kt.astype(BF16)
        ending = jnp.exp(lanes(a_row(b), BLK) - c_row(b))
        piece = dot((ending * kt).astype(BF16), v_ref[span(b), :])
        state = jnp.exp(a_row(b)) * state + piece
        own = own + a_row(b)
    tx_ref[0, :width, :] = state
    tx_ref[0, width:, :] = jnp.broadcast_to(own, (8, width))

    pl.semaphore_wait(barrier, n_seq - 1 + n_head - 1)

    def hop(way, d):
        target = seq + d if way == 0 else seq - d
        return pltpu.make_async_remote_copy(
            src_ref=tx_ref.at[way],
            dst_ref=rx_ref.at[way, d - 1],
            send_sem=send_sem.at[way, d - 1],
            recv_sem=recv_sem.at[way, d - 1],
            device_id={"seq": lax.rem(target + n_seq, n_seq)},
            device_id_type=MESH,
        )

    def reaches(way, d):
        return seq + d < n_seq if way == 0 else seq >= d

    def comes(way, d):
        return reaches(1 - way, d)

    def send(way):
        for d in range(n_seq - 1, 0, -1):
            @pl.when(reaches(way, d))
            def _():
                hop(way, d).start()

    def receive(way):
        edge_ref[:width, :] = jnp.zeros((width, width), F32)
        edge_ref[width:, :] = jnp.zeros((8, width), F32)
        for d in range(1, n_seq):
            @pl.when(comes(way, d))
            def _():
                hop(way, d).wait_recv()
                log = edge_ref[width:width + 1, :]
                edge_ref[:width, :] += jnp.exp(log) * rx_ref[way, d - 1, :width, :]
                edge_ref[width:, :] += rx_ref[way, d - 1, width:, :]
        return edge_ref[:width, :]

    def finish(way):
        for d in range(1, n_seq):
            @pl.when(reaches(way, d))
            def _():
                hop(way, d).wait_send()

    send(0)

    loads[2].wait()
    gain_col = jnp.transpose(jnp.broadcast_to(gain_ref[...], (width, width)))
    diagonal = lax.broadcasted_iota(jnp.int32, (TILE, TILE), 0) <= lax.broadcasted_iota(
        jnp.int32, (TILE, TILE), 1
    )
    for b in range(nblk):
        vt_ref[:, span(b)] = flip(v_ref[span(b), :]).astype(BF16)
        qt = flip(q_ref[span(b), :])
        qt_ref[:, span(b)] = qt.astype(BF16)
        queried_ref[:, span(b)] = (jnp.exp(c_row(b)) * qt).astype(BF16)
        col_ref[span(b), :] = jnp.transpose(jnp.broadcast_to(c_row(b), (width, BLK)))
        for i in range(tiles):
            s0 = i * TILE
            rest = BLK - s0
            scores = dot(k_ref[span(b, s0, TILE), :], q_ref[span(b, s0, rest), :], 1, 1)
            diff = c_ref[b:b + 1, s0:] - lanes(col_ref[span(b, s0, TILE), :], rest)
            near = jnp.exp(jnp.where(diagonal, diff[:, :TILE], -jnp.inf))
            inner = near
            if rest > TILE:
                inner = jnp.concatenate([near, jnp.exp(diff[:, TILE:])], axis=1)
            inner_ref[b, s0:s0 + TILE, s0:] = inner
            mix = (inner * scores).astype(BF16)
            mix_ref[b, s0:s0 + TILE, s0:] = mix
            part = dot(vt_ref[:, span(b, s0, TILE)], mix)
            if i == 0:
                out_ref[:, span(b)] = part
            else:
                out_ref[:, span(b, s0, rest)] += part
    loads[3].wait()
    for b in range(nblk):
        scaled_ref[:, span(b)] = lanes(gain_col, BLK) * flip(y_ref[span(b), :])

    entering = receive(0)
    before = jnp.zeros((1, width), F32)
    if stat_ref.shape[0] > 2 * nblk:
        stat_ref[...] = jnp.zeros_like(stat_ref)
    for b in range(nblk):
        held = state_ref[b] + jnp.exp(before) * entering
        before = before + a_row(b)
        held_ref[b] = held.astype(BF16)
        carried = dot(jnp.transpose(held).astype(BF16), qt_ref[:, span(b)])
        out = out_ref[:, span(b)] + jnp.exp(c_row(b)) * carried
        out_ref[:, span(b)] = out
        stat_ref[b:b + 1, :] = jnp.sum(out * out, axis=0, keepdims=True)
        stat_ref[nblk + b:nblk + b + 1, :] = jnp.sum(
            out * scaled_ref[:, span(b)], axis=0, keepdims=True
        )

    def share(d):
        return pltpu.make_async_remote_copy(
            src_ref=stat_ref,
            dst_ref=stats_ref.at[d - 1],
            send_sem=hsend_sem.at[d - 1],
            recv_sem=hrecv_sem.at[d - 1],
            device_id={"head": lax.rem(head + d, n_head)},
            device_id_type=MESH,
        )

    for d in range(1, n_head):
        share(d).start()
    total = stat_ref[...]
    for d in range(1, n_head):
        share(d).wait_recv()
        total = total + stats_ref[d - 1]
    inv = lax.rsqrt(total[:nblk] / features + EPS)
    coef = inv * inv * inv * total[nblk:2 * nblk] / features

    rear = jnp.zeros((width, width), F32)
    for b in reversed(range(nblk)):
        dout = (
            inv[b:b + 1] * scaled_ref[:, span(b)] - out_ref[:, span(b)] * coef[b:b + 1]
        ).astype(BF16)
        dout_ref[:, span(b)] = dout
        rear_ref[b] = rear
        rear = jnp.exp(a_row(b)) * rear + dot(queried_ref[:, span(b)], dout, 1, 1)
    tx_ref[1, :width, :] = rear
    tx_ref[1, width:, :] = jnp.broadcast_to(own, (8, width))
    send(1)

    stores = [
        [
            pltpu.make_async_copy(src.at[span(b), :], dst.at[span(b), :], out_sem.at[j, b])
            for b in range(nblk)
        ]
        for j, (src, dst) in enumerate(((oq_ref, gq_hbm), (ok_ref, gk_hbm), (ov_ref, gv_hbm)))
    ]

    for b in range(nblk):
        grad_q = jnp.exp(c_row(b)) * dot(held_ref[b], dout_ref[:, span(b)])
        halves = [grad_q[:, i * TILE:(i + 1) * TILE] for i in range(tiles)]
        for i in range(tiles):
            s0 = i * TILE
            rest = BLK - s0
            dout = dout_ref[:, span(b, s0, rest)]
            dscores = dot(v_ref[span(b, s0, TILE), :], dout)
            dmix = (inner_ref[b, s0:s0 + TILE, s0:] * dscores).astype(BF16)
            part = dot(kt_ref[:, span(b, s0, TILE)], dmix)
            for j in range(i, tiles):
                halves[j] = halves[j] + part[:, (j - i) * TILE:(j - i + 1) * TILE]
            gk_ref[span(b, s0, TILE), :] = dot(dmix, q_ref[span(b, s0, rest), :])
            gv_ref[span(b, s0, TILE), :] = dot(mix_ref[b, s0:s0 + TILE, s0:], dout, 1, 1)
        for i in range(tiles):
            oq_ref[span(b, i * TILE, TILE), :] = jnp.transpose(halves[i]).astype(BF16)
        stores[0][b].start()
        col_ref[span(b), :] = jnp.exp(a_row(b) - col_ref[span(b), :])

    leaving = receive(1)
    after = jnp.zeros((1, width), F32)
    for b in reversed(range(nblk)):
        kept = (rear_ref[b] + jnp.exp(after) * leaving).astype(BF16)
        after = after + a_row(b)
        ending = col_ref[span(b), :]
        ok_ref[span(b), :] = (
            gk_ref[span(b), :] + ending * dot(v_ref[span(b), :], kept, 1, 1)
        ).astype(BF16)
        stores[1][b].start()
        ov_ref[span(b), :] = (
            gv_ref[span(b), :] + ending * dot(k_ref[span(b), :], kept)
        ).astype(BF16)
        stores[2][b].start()

    finish(0)
    finish(1)
    for d in range(1, n_head):
        share(d).wait_send()
    for row in stores:
        for store in row:
            store.wait()


def shards(n_seq, n_head, query, key, value, grad_out, log_decay, gain):
    tokens, width = query.shape
    nblk = tokens // BLK
    features = width * n_head
    rows = -(-nblk // 8) * 8
    srows = -(-2 * nblk // 8) * 8
    big = lambda dtype: pltpu.VMEM((tokens, width), dtype)
    wide = lambda dtype: pltpu.VMEM((width, tokens), dtype)
    shape = jax.ShapeDtypeStruct((tokens, width), BF16)
    hbm = pl.BlockSpec(memory_space=pl.ANY)
    vmem = pl.BlockSpec(memory_space=pltpu.VMEM)
    dma = pltpu.SemaphoreType.DMA
    return pl.pallas_call(
        functools.partial(kernel, n_seq, n_head, features),
        out_shape=(shape, shape, shape),
        in_specs=[hbm] * 4 + [vmem] * 2,
        out_specs=(hbm, hbm, hbm),
        scratch_shapes=[
            big(BF16), big(BF16), big(BF16), big(BF16),
            wide(BF16), wide(BF16), wide(BF16), wide(BF16), wide(F32),
            pltpu.VMEM((rows, BLK), F32),
            pltpu.VMEM((rows, width), F32),
            big(F32),
            pltpu.VMEM((nblk, BLK, BLK), F32),
            pltpu.VMEM((nblk, BLK, BLK), BF16),
            wide(F32), wide(BF16),
            pltpu.VMEM((nblk, width, width), F32),
            pltpu.VMEM((nblk, width, width), F32),
            pltpu.VMEM((nblk, width, width), BF16),
            big(F32), big(F32), big(BF16), big(BF16), big(BF16),
            pltpu.VMEM((width + 8, width), F32),
            pltpu.VMEM((2, width + 8, width), F32),
            pltpu.VMEM((2, n_seq - 1, width + 8, width), F32),
            pltpu.VMEM((srows, BLK), F32),
            pltpu.VMEM((n_head - 1, srows, BLK), F32),
            dma((4,)), dma((3, nblk)),
            dma((2, n_seq - 1)), dma((2, n_seq - 1)),
            dma((n_head - 1,)), dma((n_head - 1,)),
        ],
        compiler_params=pltpu.CompilerParams(collective_id=0, has_side_effects=True),
    )(query, key, value, grad_out, log_decay, gain.reshape(1, width))


def solution(mesh):
    return jax.shard_map(
        functools.partial(shards, mesh.shape["seq"], mesh.shape["head"]),
        mesh=mesh,
        in_specs=(
            P("seq", "head"),
            P("seq", "head"),
            P("seq", "head"),
            P("seq", "head"),
            P("head", "seq"),
            P("head"),
        ),
        out_specs=(P("seq", "head"), P("seq", "head"), P("seq", "head")),
        check_vma=False,
    )
```

profile of v0, /device:TPU:0, one launch (start us, length us, event | category | flops | bytes accessed | tf_op | source)
XLA Modules:
  0.0 31.1 jit_solution(18101242152618110913)
XLA Ops:
  0.6 26.5 %shard_map.85 = (bf16[2048,128]{1,0:T(8,128)(2,1)}, bf16[2048,128]{1,0:T(8,128)(2,1)}, bf16[2048,128]{1,0:T(8,128)(2,1)}) custom-call(bf16[2048,128]{1,0:T(8,128)(2,1)} %q_hbm.1, bf16[2048,128]{1,0:T(8,128)(2,1)} %k_hbm.1, bf16[2048,128]{1,0:T(8,128)(2,1)} %v_hbm.1, bf16[2048,128]{1,0:T(8,128)(2,1)} %y_hbm.1, f32[1,2048]{1,0:T(1,128)} %decay_ref.1, ...), custom_call_target="tpu_custom_call" | custom-call | tf_op jit(solution)/shard_map/pallas_call | solution.py:298
  27.2 0.0 copy-start.1
  27.2 1.9 %copy.12 = bf16[2048,128]{1,0:T(8,128)(2,1)} copy(bf16[2048,128]{1,0:T(8,128)(2,1)} %get-tuple-element.6) | data formatting | bytes 1048576
  29.1 0.0 copy-done.1
  29.1 0.0 copy-start
  29.1 0.8 %copy.13 = bf16[2048,128]{1,0:T(8,128)(2,1)} copy(bf16[2048,128]{1,0:T(8,128)(2,1)S(1)} %copy-done.1) | data formatting | bytes 1048576
  29.9 0.4 %copy-done = bf16[2048,128]{1,0:T(8,128)(2,1)S(1)} copy-done((bf16[2048,128]{1,0:T(8,128)(2,1)S(1)}, bf16[2048,128]{1,0:T(8,128)(2,1)}, u32[]{:S(2)}) %copy-start) | copy-done | bytes 524312
  30.4 0.8 %copy.14 = bf16[2048,128]{1,0:T(8,128)(2,1)} copy(bf16[2048,128]{1,0:T(8,128)(2,1)S(1)} %copy-done) | data formatting | bytes 1048576
Async XLA Ops:
  27.2 1.9 %copy-start.1 = (bf16[2048,128]{1,0:T(8,128)(2,1)S(1)}, bf16[2048,128]{1,0:T(8,128)(2,1)}, u32[]{:S(2)}) copy-start(bf16[2048,128]{1,0:T(8,128)(2,1)} %get-tuple-element.7) | copy-start | bytes 1572868
  29.1 1.2 %copy-start = (bf16[2048,128]{1,0:T(8,128)(2,1)S(1)}, bf16[2048,128]{1,0:T(8,128)(2,1)}, u32[]{:S(2)}) copy-start(bf16[2048,128]{1,0:T(8,128)(2,1)} %get-tuple-element.8) | copy-start | bytes 1572868
where the time goes:
time: 31.4 us; the launch traced here: 31.1 us
  Pallas kernels  26.5 us (84%)
  local copies, waits for them, and re-layouts  3.95 us (13%)
  between operations  0.65 us (2%)
    pallas_call x1, Pallas kernels, shards(): pl.pallas_call(functools.partial(kernel, n_seq, n_head, features), out_sh...  26.5 us
    unnamed x7, local copies, waits for them, and re-layouts  3.95 us

commit v1 on v0

--- a/solution.py
+++ b/solution.py
@@ -31,13 +31,13 @@
 
 def kernel(
     n_seq, n_head, features,
-    q_hbm, k_hbm, v_hbm, y_hbm, decay_ref, gain_ref,
-    gq_hbm, gk_hbm, gv_hbm,
-    q_ref, k_ref, v_ref, y_ref, kt_ref, qt_ref, vt_ref, queried_ref, scaled_ref,
+    q_hbm, k_hbm, v_hbm, y_hbm, decay_hbm, gain_hbm,
+    oq_ref, k_ref, v_ref, gk_ref, gv_ref, end_ref, kept_ref,
+    decay_ref, gain_ref, q_ref, y_ref, kt_ref, qt_ref, vt_ref, queried_ref, scaled_ref,
     c_ref, a_ref, col_ref, inner_ref, mix_ref, out_ref, dout_ref,
-    state_ref, rear_ref, held_ref, gk_ref, gv_ref, oq_ref, ok_ref, ov_ref, edge_ref,
+    state_ref, rear_ref, held_ref, edge_ref,
     tx_ref, rx_ref, stat_ref, stats_ref,
-    in_sem, out_sem, send_sem, recv_sem, hsend_sem, hrecv_sem,
+    in_sem, send_sem, recv_sem, hsend_sem, hrecv_sem,
 ):
     seq = lax.axis_index("seq")
     head = lax.axis_index("head")
@@ -45,15 +45,6 @@
     nblk = tokens // BLK
     tiles = BLK // TILE
 
-    loads = [
-        pltpu.make_async_copy(src, dst, in_sem.at[i])
-        for i, (src, dst) in enumerate(
-            ((k_hbm, k_ref), (v_hbm, v_ref), (q_hbm, q_ref), (y_hbm, y_ref))
-        )
-    ]
-    for load in loads:
-        load.start()
-
     barrier = pltpu.get_barrier_semaphore()
     for d in range(1, n_seq):
         pl.semaphore_signal(
@@ -64,10 +55,27 @@
             barrier, inc=1, device_id={"head": lax.rem(head + d, n_head)}, device_id_type=MESH
         )
 
+    pairs = [(decay_hbm, decay_ref)]
+    for b in range(nblk):
+        part = pl.ds(b * BLK, BLK)
+        pairs += [(k_hbm.at[part, :], k_ref.at[part, :]), (v_hbm.at[part, :], v_ref.at[part, :])]
+    pairs += [(q_hbm, q_ref), (y_hbm, y_ref), (gain_hbm, gain_ref)]
+    loads = [
+        pltpu.make_async_copy(src, dst, in_sem.at[i]) for i, (src, dst) in enumerate(pairs)
+    ]
+    for load in loads:
+        load.start()
+
     def span(b, start=0, size=BLK):
         return pl.ds(b * BLK + start, size)
 
+    upper = jnp.where(
+        lax.broadcasted_iota(jnp.int32, (BLK, BLK), 0)
+        <= lax.broadcasted_iota(jnp.int32, (BLK, BLK), 1),
+        1.0, 0.0,
+    ).astype(BF16)
     rows = c_ref.shape[0]
+    loads[0].wait()
     x = jnp.concatenate(
         [decay_ref[:, b * BLK:(b + 1) * BLK] for b in range(nblk)]
         + ([jnp.zeros((rows - nblk, BLK), F32)] if rows > nblk else []),
@@ -77,11 +85,6 @@
     x2 = (x - x1).astype(BF16).astype(F32)
     x3 = x - x1 - x2
     parts = jnp.concatenate([x1, x2, x3, jnp.zeros_like(x)], axis=0).astype(BF16)
-    upper = jnp.where(
-        lax.broadcasted_iota(jnp.int32, (BLK, BLK), 0)
-        <= lax.broadcasted_iota(jnp.int32, (BLK, BLK), 1),
-        1.0, 0.0,
-    ).astype(BF16)
     sums = dot(parts, upper)
     c_all = sums[:rows] + sums[rows:2 * rows] + sums[2 * rows:3 * rows]
     c_ref[...] = c_all
@@ -93,11 +96,11 @@
     def a_row(b):
         return a_ref[b:b + 1, :]
 
-    loads[0].wait()
-    loads[1].wait()
     state = jnp.zeros((width, width), F32)
     own = jnp.zeros((1, width), F32)
     for b in range(nblk):
+        loads[1 + 2 * b].wait()
+        loads[2 + 2 * b].wait()
         state_ref[b] = state
         kt = flip(k_ref[span(b), :])
         kt_ref[:, span(b)] = kt.astype(BF16)
@@ -153,7 +156,8 @@
 
     send(0)
 
-    loads[2].wait()
+    loads[2 * nblk + 1].wait()
+    loads[2 * nblk + 3].wait()
     gain_col = jnp.transpose(jnp.broadcast_to(gain_ref[...], (width, width)))
     diagonal = lax.broadcasted_iota(jnp.int32, (TILE, TILE), 0) <= lax.broadcasted_iota(
         jnp.int32, (TILE, TILE), 1
@@ -181,7 +185,7 @@
                 out_ref[:, span(b)] = part
             else:
                 out_ref[:, span(b, s0, rest)] += part
-    loads[3].wait()
+    loads[2 * nblk + 2].wait()
     for b in range(nblk):
         scaled_ref[:, span(b)] = lanes(gain_col, BLK) * flip(y_ref[span(b), :])
 
@@ -231,14 +235,6 @@
     tx_ref[1, :width, :] = rear
     tx_ref[1, width:, :] = jnp.broadcast_to(own, (8, width))
     send(1)
-
-    stores = [
-        [
-            pltpu.make_async_copy(src.at[span(b), :], dst.at[span(b), :], out_sem.at[j, b])
-            for b in range(nblk)
-        ]
-        for j, (src, dst) in enumerate(((oq_ref, gq_hbm), (ok_ref, gk_hbm), (ov_ref, gv_hbm)))
-    ]
 
     for b in range(nblk):
         grad_q = jnp.exp(c_row(b)) * dot(held_ref[b], dout_ref[:, span(b)])
@@ -256,31 +252,51 @@
             gv_ref[span(b, s0, TILE), :] = dot(mix_ref[b, s0:s0 + TILE, s0:], dout, 1, 1)
         for i in range(tiles):
             oq_ref[span(b, i * TILE, TILE), :] = jnp.transpose(halves[i]).astype(BF16)
-        stores[0][b].start()
-        col_ref[span(b), :] = jnp.exp(a_row(b) - col_ref[span(b), :])
+        end_ref[span(b), :] = jnp.exp(a_row(b) - col_ref[span(b), :])
 
     leaving = receive(1)
     after = jnp.zeros((1, width), F32)
     for b in reversed(range(nblk)):
-        kept = (rear_ref[b] + jnp.exp(after) * leaving).astype(BF16)
+        kept_ref[b] = (rear_ref[b] + jnp.exp(after) * leaving).astype(BF16)
         after = after + a_row(b)
-        ending = col_ref[span(b), :]
-        ok_ref[span(b), :] = (
-            gk_ref[span(b), :] + ending * dot(v_ref[span(b), :], kept, 1, 1)
-        ).astype(BF16)
-        stores[1][b].start()
-        ov_ref[span(b), :] = (
-            gv_ref[span(b), :] + ending * dot(k_ref[span(b), :], kept)
-        ).astype(BF16)
-        stores[2][b].start()
 
     finish(0)
     finish(1)
     for d in range(1, n_head):
         share(d).wait_send()
-    for row in stores:
-        for store in row:
-            store.wait()
+
+
+def closing(
+    oq_ref, k_ref, v_ref, gk_ref, gv_ref, end_ref, kept_ref,
+    gq_hbm, gk_hbm, gv_hbm,
+    ok_ref, ov_ref, out_sem,
+):
+    tokens = k_ref.shape[0]
+    nblk = tokens // BLK
+
+    def span(b):
+        return pl.ds(b * BLK, BLK)
+
+    first = pltpu.make_async_copy(oq_ref, gq_hbm, out_sem.at[2 * nblk])
+    first.start()
+    stores = []
+    for b in range(nblk):
+        ending = end_ref[span(b), :]
+        ok_ref[span(b), :] = (
+            gk_ref[span(b), :] + ending * dot(v_ref[span(b), :], kept_ref[b], 1, 1)
+        ).astype(BF16)
+        ov_ref[span(b), :] = (
+            gv_ref[span(b), :] + ending * dot(k_ref[span(b), :], kept_ref[b])
+        ).astype(BF16)
+        for i, (src, dst) in enumerate(((ok_ref, gk_hbm), (ov_ref, gv_hbm))):
+            store = pltpu.make_async_copy(
+                src.at[span(b), :], dst.at[span(b), :], out_sem.at[2 * b + i]
+            )
+            store.start()
+            stores.append(store)
+    first.wait()
+    for store in stores:
+        store.wait()
 
 
 def shards(n_seq, n_head, query, key, value, grad_out, log_decay, gain):
@@ -295,13 +311,16 @@
     hbm = pl.BlockSpec(memory_space=pl.ANY)
     vmem = pl.BlockSpec(memory_space=pltpu.VMEM)
     dma = pltpu.SemaphoreType.DMA
-    return pl.pallas_call(
+    kept = pltpu.VMEM((nblk, width, width), BF16)
+    stay = lambda x: pltpu.with_memory_space_constraint(x, pltpu.HBM)
+    middle = pl.pallas_call(
         functools.partial(kernel, n_seq, n_head, features),
-        out_shape=(shape, shape, shape),
-        in_specs=[hbm] * 4 + [vmem] * 2,
-        out_specs=(hbm, hbm, hbm),
+        out_shape=(big(BF16), big(BF16), big(BF16), big(F32), big(F32), big(F32), kept),
+        in_specs=[pl.BlockSpec(memory_space=pltpu.HBM)] * 6,
+        out_specs=(vmem,) * 7,
         scratch_shapes=[
-            big(BF16), big(BF16), big(BF16), big(BF16),
+            pltpu.VMEM((1, tokens), F32), pltpu.VMEM((1, width), F32),
+            big(BF16), big(BF16),
             wide(BF16), wide(BF16), wide(BF16), wide(BF16), wide(F32),
             pltpu.VMEM((rows, BLK), F32),
             pltpu.VMEM((rows, width), F32),
@@ -312,18 +331,27 @@
             pltpu.VMEM((nblk, width, width), F32),
             pltpu.VMEM((nblk, width, width), F32),
             pltpu.VMEM((nblk, width, width), BF16),
-            big(F32), big(F32), big(BF16), big(BF16), big(BF16),
             pltpu.VMEM((width + 8, width), F32),
             pltpu.VMEM((2, width + 8, width), F32),
             pltpu.VMEM((2, n_seq - 1, width + 8, width), F32),
             pltpu.VMEM((srows, BLK), F32),
             pltpu.VMEM((n_head - 1, srows, BLK), F32),
-            dma((4,)), dma((3, nblk)),
+            dma((2 * nblk + 4,)),
             dma((2, n_seq - 1)), dma((2, n_seq - 1)),
             dma((n_head - 1,)), dma((n_head - 1,)),
         ],
-        compiler_params=pltpu.CompilerParams(collective_id=0, has_side_effects=True),
-    )(query, key, value, grad_out, log_decay, gain.reshape(1, width))
+        compiler_params=pltpu.CompilerParams(
+            collective_id=0, has_side_effects=True, vmem_limit_bytes=40 << 20
+        ),
+    )(*map(stay, (query, key, value, grad_out, log_decay, gain.reshape(1, width))))
+    return pl.pallas_call(
+        closing,
+        out_shape=(shape, shape, shape),
+        in_specs=[vmem] * 7,
+        out_specs=(hbm, hbm, hbm),
+        scratch_shapes=[big(BF16), big(BF16), dma((2 * nblk + 1,))],
+        compiler_params=pltpu.CompilerParams(vmem_limit_bytes=8 << 20),
+    )(*middle)
 
 
 def solution(mesh):

time: 31.4 us -> 26.8 us (0.85)
  local copies, waits for them, and re-layouts: 3.95 us -> 0 us
  Pallas kernels: 26.5 us -> 25.9 us
    unnamed x7 -> x0, local copies, waits for them, and re-layouts: 3.95 us -> none
    pallas_call x1, Pallas kernels: 26.5 us -> 24.7 us  [shards(): pl.pallas_call(functools.partial(kernel, n_seq, n_head, features), out_sh...]
    pallas_call x0 -> x1, Pallas kernels: none -> 1.26 us  [shards(): pl.pallas_call(closing, out_shape=(shape, shape, shape), in_specs=[vmem]...]
where the time goes in v1:
time: 26.8 us; the launch traced here: 26.6 us
  Pallas kernels  25.9 us (97%)
  between operations  0.64 us (2%)
    pallas_call x1, Pallas kernels, shards(): pl.pallas_call(functools.partial(kernel, n_seq, n_head, features), out_sh...  24.7 us
    pallas_call x1, Pallas kernels, shards(): pl.pallas_call(closing, out_shape=(shape, shape, shape), in_specs=[vmem]...  1.26 us

profile of v1, /device:TPU:0, one launch (start us, length us, event | category | flops | bytes accessed | tf_op | source)
XLA Modules:
  0.0 26.6 jit_solution(1324046989117703426)
XLA Ops:
  0.6 24.7 %shard_map.85 = (bf16[2048,128]{1,0:T(8,128)(2,1)S(1)}, bf16[2048,128]{1,0:T(8,128)(2,1)S(1)}, bf16[2048,128]{1,0:T(8,128)(2,1)S(1)}, f32[2048,128]{1,0:T(8,128)...) custom-call(bf16[2048,128]{1,0:T(8,128)(2,1)} %q_hbm.1, ...), custom_call_target="tpu_custom_call" | custom-call | tf_op jit(solution)/shard_map/pallas_call | solution.py:316
  25.3 1.3 %shard_map.86 = (bf16[2048,128]{1,0:T(8,128)(2,1)}, bf16[2048,128]{1,0:T(8,128)(2,1)}, bf16[2048,128]{1,0:T(8,128)(2,1)}) custom-call(bf16[2048,128]{1,0:T(8,128)(2,1)S(1)} %get-tuple-element.10.oq_ref, bf16[2048,128]{1,0:T(8,128)(2,1)S(1)} %get-tuple-element.11.k_ref, bf16[2048,128]{1,0:T(8,128)(2,1)S(1)} %get-tuple-element.12.v_ref, ...), custom_call_target="tpu_custom_call" | custom-call | tf_op jit(solution)/shard_map/pallas_call | solution.py:347

commit v2 on v1

--- a/solution.py
+++ b/solution.py
@@ -131,7 +131,7 @@
         return reaches(1 - way, d)
 
     def send(way):
-        for d in range(n_seq - 1, 0, -1):
+        for d in range(1, n_seq) if way == 0 else range(n_seq - 1, 0, -1):
             @pl.when(reaches(way, d))
             def _():
                 hop(way, d).start()

time: 26.8 us -> 25.1 us (0.937)
  Pallas kernels: 25.9 us -> 24.3 us
    pallas_call x1, Pallas kernels: 24.7 us -> 23 us  [shards(): pl.pallas_call(functools.partial(kernel, n_seq, n_head, features), out_sh...]
where the time goes in v2:
time: 25.1 us; the launch traced here: 24.9 us
  Pallas kernels  24.3 us (97%)
  between operations  0.64 us (3%)
    pallas_call x1, Pallas kernels, shards(): pl.pallas_call(functools.partial(kernel, n_seq, n_head, features), out_sh...  23 us
    pallas_call x1, Pallas kernels, shards(): pl.pallas_call(closing, out_shape=(shape, shape, shape), in_specs=[vmem]...  1.26 us

profile of v2, /device:TPU:0, one launch (start us, length us, event | category | flops | bytes accessed | tf_op | source)
XLA Modules:
  0.0 24.9 jit_solution(12157170958011643247)
XLA Ops:
  0.6 23.0 %shard_map.85 = (bf16[2048,128]{1,0:T(8,128)(2,1)S(1)}, bf16[2048,128]{1,0:T(8,128)(2,1)S(1)}, bf16[2048,128]{1,0:T(8,128)(2,1)S(1)}, f32[2048,128]{1,0:T(8,128)...) custom-call(bf16[2048,128]{1,0:T(8,128)(2,1)} %q_hbm.1, ...), custom_call_target="tpu_custom_call" | custom-call | tf_op jit(solution)/shard_map/pallas_call | solution.py:316
  23.6 1.3 %shard_map.86 = (bf16[2048,128]{1,0:T(8,128)(2,1)}, bf16[2048,128]{1,0:T(8,128)(2,1)}, bf16[2048,128]{1,0:T(8,128)(2,1)}) custom-call(bf16[2048,128]{1,0:T(8,128)(2,1)S(1)} %get-tuple-element.10.oq_ref, bf16[2048,128]{1,0:T(8,128)(2,1)S(1)} %get-tuple-element.11.k_ref, bf16[2048,128]{1,0:T(8,128)(2,1)S(1)} %get-tuple-element.12.v_ref, ...), custom_call_target="tpu_custom_call" | custom-call | tf_op jit(solution)/shard_map/pallas_call | solution.py:347

commit v3 on v2

--- a/solution.py
+++ b/solution.py
@@ -36,7 +36,7 @@
     decay_ref, gain_ref, q_ref, y_ref, kt_ref, qt_ref, vt_ref, queried_ref, scaled_ref,
     c_ref, a_ref, col_ref, inner_ref, mix_ref, out_ref, dout_ref,
     state_ref, rear_ref, held_ref, edge_ref,
-    tx_ref, rx_ref, stat_ref, stats_ref,
+    tx_ref, rx_ref, back_ref, rear_rx_ref, scale_ref, stat_ref, stats_ref,
     in_sem, send_sem, recv_sem, hsend_sem, hrecv_sem,
 ):
     seq = lax.axis_index("seq")
@@ -56,9 +56,10 @@
         )
 
     pairs = [(decay_hbm, decay_ref)]
-    for b in range(nblk):
-        part = pl.ds(b * BLK, BLK)
-        pairs += [(k_hbm.at[part, :], k_ref.at[part, :]), (v_hbm.at[part, :], v_ref.at[part, :])]
+    for src, dst in ((k_hbm, k_ref), (v_hbm, v_ref)):
+        for b in range(nblk):
+            part = pl.ds(b * BLK, BLK)
+            pairs.append((src.at[part, :], dst.at[part, :]))
     pairs += [(q_hbm, q_ref), (y_hbm, y_ref), (gain_hbm, gain_ref)]
     loads = [
         pltpu.make_async_copy(src, dst, in_sem.at[i]) for i, (src, dst) in enumerate(pairs)
@@ -69,26 +70,44 @@
     def span(b, start=0, size=BLK):
         return pl.ds(b * BLK + start, size)
 
+    rows = c_ref.shape[0]
     upper = jnp.where(
-        lax.broadcasted_iota(jnp.int32, (BLK, BLK), 0)
-        <= lax.broadcasted_iota(jnp.int32, (BLK, BLK), 1),
+        lax.broadcasted_iota(jnp.int32, (width, width), 0)
+        <= lax.broadcasted_iota(jnp.int32, (width, width), 1),
         1.0, 0.0,
     ).astype(BF16)
-    rows = c_ref.shape[0]
+    pieces = BLK // width
+    pad = [jnp.zeros((rows - nblk, width), F32)] if rows > nblk else []
     loads[0].wait()
+    for b in range(nblk):
+        loads[1 + b].wait()
+        loads[1 + nblk + b].wait()
     x = jnp.concatenate(
-        [decay_ref[:, b * BLK:(b + 1) * BLK] for b in range(nblk)]
-        + ([jnp.zeros((rows - nblk, BLK), F32)] if rows > nblk else []),
+        sum(
+            (
+                [
+                    decay_ref[:, b * BLK + j * width:b * BLK + (j + 1) * width]
+                    for b in range(nblk)
+                ]
+                + pad
+                for j in range(pieces)
+            ),
+            [],
+        ),
         axis=0,
     )
     x1 = x.astype(BF16).astype(F32)
     x2 = (x - x1).astype(BF16).astype(F32)
     x3 = x - x1 - x2
-    parts = jnp.concatenate([x1, x2, x3, jnp.zeros_like(x)], axis=0).astype(BF16)
-    sums = dot(parts, upper)
-    c_all = sums[:rows] + sums[rows:2 * rows] + sums[2 * rows:3 * rows]
-    c_ref[...] = c_all
-    a_ref[...] = jnp.broadcast_to(c_all[:, BLK - 1:BLK], (rows, width))
+    sums = dot(jnp.concatenate([x1, x2, x3], axis=0).astype(BF16), upper)
+    size = pieces * rows
+    sums = sums[:size] + sums[size:2 * size] + sums[2 * size:]
+    total = jnp.zeros((rows, width), F32)
+    for j in range(pieces):
+        piece = sums[j * rows:(j + 1) * rows]
+        c_ref[:, j * width:(j + 1) * width] = piece + total
+        total = total + jnp.broadcast_to(piece[:, width - 1:], (rows, width))
+    a_ref[...] = total
 
     def c_row(b):
         return c_ref[b:b + 1, :]
@@ -96,28 +115,32 @@
     def a_row(b):
         return a_ref[b:b + 1, :]
 
-    state = jnp.zeros((width, width), F32)
-    own = jnp.zeros((1, width), F32)
-    for b in range(nblk):
-        loads[1 + 2 * b].wait()
-        loads[2 + 2 * b].wait()
-        state_ref[b] = state
+    keyed = []
+    for b in range(nblk):
         kt = flip(k_ref[span(b), :])
         kt_ref[:, span(b)] = kt.astype(BF16)
         ending = jnp.exp(lanes(a_row(b), BLK) - c_row(b))
-        piece = dot((ending * kt).astype(BF16), v_ref[span(b), :])
-        state = jnp.exp(a_row(b)) * state + piece
+        keyed.append((ending * kt).astype(BF16))
+    state = jnp.zeros((width, width), F32)
+    own = jnp.zeros((1, width), F32)
+    for b in range(nblk):
+        state_ref[b] = state
+        state = jnp.exp(a_row(b)) * state + dot(keyed[b], v_ref[span(b), :])
         own = own + a_row(b)
-    tx_ref[0, :width, :] = state
-    tx_ref[0, width:, :] = jnp.broadcast_to(own, (8, width))
+    tx_ref[:width, :] = state
+    tx_ref[width:, :] = jnp.broadcast_to(own, (8, width))
 
     pl.semaphore_wait(barrier, n_seq - 1 + n_head - 1)
 
     def hop(way, d):
-        target = seq + d if way == 0 else seq - d
+        if way == 0:
+            head_rows = pl.ds(0, width + 1)
+            target, src, dst = seq + d, tx_ref.at[head_rows, :], rx_ref.at[d - 1, head_rows, :]
+        else:
+            target, src, dst = seq - d, back_ref.at[d - 1], rear_rx_ref.at[d - 1]
         return pltpu.make_async_remote_copy(
-            src_ref=tx_ref.at[way],
-            dst_ref=rx_ref.at[way, d - 1],
+            src_ref=src,
+            dst_ref=dst,
             send_sem=send_sem.at[way, d - 1],
             recv_sem=recv_sem.at[way, d - 1],
             device_id={"seq": lax.rem(target + n_seq, n_seq)},
@@ -130,23 +153,34 @@
     def comes(way, d):
         return reaches(1 - way, d)
 
-    def send(way):
-        for d in range(1, n_seq) if way == 0 else range(n_seq - 1, 0, -1):
-            @pl.when(reaches(way, d))
-            def _():
-                hop(way, d).start()
-
-    def receive(way):
+    def receive():
         edge_ref[:width, :] = jnp.zeros((width, width), F32)
         edge_ref[width:, :] = jnp.zeros((8, width), F32)
         for d in range(1, n_seq):
-            @pl.when(comes(way, d))
+            @pl.when(comes(0, d))
             def _():
-                hop(way, d).wait_recv()
+                hop(0, d).wait_recv()
                 log = edge_ref[width:width + 1, :]
-                edge_ref[:width, :] += jnp.exp(log) * rx_ref[way, d - 1, :width, :]
-                edge_ref[width:, :] += rx_ref[way, d - 1, width:, :]
+                scale_ref[d - 1:d, :] = log
+                edge_ref[:width, :] += jnp.exp(log) * rx_ref[d - 1, :width, :]
+                edge_ref[width:width + 1, :] += rx_ref[d - 1, width:width + 1, :]
         return edge_ref[:width, :]
+
+    def receive_back():
+        edge_ref[:width, :] = jnp.zeros((width, width), F32)
+        for d in range(1, n_seq):
+            @pl.when(comes(1, d))
+            def _():
+                hop(1, d).wait_recv()
+                edge_ref[:width, :] += rear_rx_ref[d - 1]
+        return edge_ref[:width, :]
+
+    def send_back(far):
+        for d in range(n_seq - 1, 0, -1):
+            @pl.when(seq == d if far else seq > d)
+            def _():
+                back_ref[d - 1] = jnp.exp(scale_ref[d - 1:d, :]) * rear_ref[nblk]
+                hop(1, d).start()
 
     def finish(way):
         for d in range(1, n_seq):
@@ -154,7 +188,10 @@
             def _():
                 hop(way, d).wait_send()
 
-    send(0)
+    for d in range(1, n_seq):
+        @pl.when(reaches(0, d))
+        def _():
+            hop(0, d).start()
 
     loads[2 * nblk + 1].wait()
     loads[2 * nblk + 3].wait()
@@ -189,7 +226,7 @@
     for b in range(nblk):
         scaled_ref[:, span(b)] = lanes(gain_col, BLK) * flip(y_ref[span(b), :])
 
-    entering = receive(0)
+    entering = receive()
     before = jnp.zeros((1, width), F32)
     if stat_ref.shape[0] > 2 * nblk:
         stat_ref[...] = jnp.zeros_like(stat_ref)
@@ -232,9 +269,8 @@
         dout_ref[:, span(b)] = dout
         rear_ref[b] = rear
         rear = jnp.exp(a_row(b)) * rear + dot(queried_ref[:, span(b)], dout, 1, 1)
-    tx_ref[1, :width, :] = rear
-    tx_ref[1, width:, :] = jnp.broadcast_to(own, (8, width))
-    send(1)
+    rear_ref[nblk] = rear
+    send_back(True)
 
     for b in range(nblk):
         grad_q = jnp.exp(c_row(b)) * dot(held_ref[b], dout_ref[:, span(b)])
@@ -253,8 +289,10 @@
         for i in range(tiles):
             oq_ref[span(b, i * TILE, TILE), :] = jnp.transpose(halves[i]).astype(BF16)
         end_ref[span(b), :] = jnp.exp(a_row(b) - col_ref[span(b), :])
-
-    leaving = receive(1)
+        if b == min(1, nblk - 1):
+            send_back(False)
+
+    leaving = receive_back()
     after = jnp.zeros((1, width), F32)
     for b in reversed(range(nblk)):
         kept_ref[b] = (rear_ref[b] + jnp.exp(after) * leaving).astype(BF16)
@@ -329,11 +367,14 @@
             pltpu.VMEM((nblk, BLK, BLK), BF16),
             wide(F32), wide(BF16),
             pltpu.VMEM((nblk, width, width), F32),
-            pltpu.VMEM((nblk, width, width), F32),
+            pltpu.VMEM((nblk + 1, width, width), F32),
             pltpu.VMEM((nblk, width, width), BF16),
             pltpu.VMEM((width + 8, width), F32),
-            pltpu.VMEM((2, width + 8, width), F32),
-            pltpu.VMEM((2, n_seq - 1, width + 8, width), F32),
+            pltpu.VMEM((width + 8, width), F32),
+            pltpu.VMEM((n_seq - 1, width + 8, width), F32),
+            pltpu.VMEM((n_seq - 1, width, width), F32),
+            pltpu.VMEM((n_seq - 1, width, width), F32),
+            pltpu.VMEM((n_seq, width), F32),
             pltpu.VMEM((srows, BLK), F32),
             pltpu.VMEM((n_head - 1, srows, BLK), F32),
             dma((2 * nblk + 4,)),

time: 25.1 us -> 24.3 us (0.968)
  Pallas kernels: 24.3 us -> 23.4 us
    pallas_call x1, Pallas kernels: 23 us -> 22.1 us  [shards(): pl.pallas_call(functools.partial(kernel, n_seq, n_head, features), out_sh...]
where the time goes in v3:
time: 24.3 us; the launch traced here: 24 us
  Pallas kernels  23.4 us (96%)
  between operations  0.64 us (3%)
    pallas_call x1, Pallas kernels, shards(): pl.pallas_call(functools.partial(kernel, n_seq, n_head, features), out_sh...  22.1 us
    pallas_call x1, Pallas kernels, shards(): pl.pallas_call(closing, out_shape=(shape, shape, shape), in_specs=[vmem]...  1.26 us

profile of v3, /device:TPU:0, one launch (start us, length us, event | category | flops | bytes accessed | tf_op | source)
XLA Modules:
  0.0 24.0 jit_solution(5335474294632837303)
XLA Ops:
  0.6 22.1 %shard_map.85 = (bf16[2048,128]{1,0:T(8,128)(2,1)S(1)}, bf16[2048,128]{1,0:T(8,128)(2,1)S(1)}, bf16[2048,128]{1,0:T(8,128)(2,1)S(1)}, f32[2048,128]{1,0:T(8,128)...) custom-call(bf16[2048,128]{1,0:T(8,128)(2,1)} %q_hbm.1, ...), custom_call_target="tpu_custom_call" | custom-call | tf_op jit(solution)/shard_map/pallas_call | solution.py:354
  22.8 1.3 %shard_map.86 = (bf16[2048,128]{1,0:T(8,128)(2,1)}, bf16[2048,128]{1,0:T(8,128)(2,1)}, bf16[2048,128]{1,0:T(8,128)(2,1)}) custom-call(bf16[2048,128]{1,0:T(8,128)(2,1)S(1)} %get-tuple-element.10.oq_ref, bf16[2048,128]{1,0:T(8,128)(2,1)S(1)} %get-tuple-element.11.k_ref, bf16[2048,128]{1,0:T(8,128)(2,1)S(1)} %get-tuple-element.12.v_ref, ...), custom_call_target="tpu_custom_call" | custom-call | tf_op jit(solution)/shard_map/pallas_call | solution.py:388

commit v4 on v3

--- a/solution.py
+++ b/solution.py
@@ -36,7 +36,7 @@
     decay_ref, gain_ref, q_ref, y_ref, kt_ref, qt_ref, vt_ref, queried_ref, scaled_ref,
     c_ref, a_ref, col_ref, inner_ref, mix_ref, out_ref, dout_ref,
     state_ref, rear_ref, held_ref, edge_ref,
-    tx_ref, rx_ref, back_ref, rear_rx_ref, scale_ref, stat_ref, stats_ref,
+    tx_ref, rx_ref, back_ref, rear_rx_ref, scale_ref, flipped_ref, scales_ref, stat_ref, stats_ref,
     in_sem, send_sem, recv_sem, hsend_sem, hrecv_sem,
 ):
     seq = lax.axis_index("seq")
@@ -55,12 +55,10 @@
             barrier, inc=1, device_id={"head": lax.rem(head + d, n_head)}, device_id_type=MESH
         )
 
-    pairs = [(decay_hbm, decay_ref)]
-    for src, dst in ((k_hbm, k_ref), (v_hbm, v_ref)):
-        for b in range(nblk):
-            part = pl.ds(b * BLK, BLK)
-            pairs.append((src.at[part, :], dst.at[part, :]))
-    pairs += [(q_hbm, q_ref), (y_hbm, y_ref), (gain_hbm, gain_ref)]
+    pairs = (
+        (decay_hbm, decay_ref), (k_hbm, k_ref), (v_hbm, v_ref), (q_hbm, q_ref), (y_hbm, y_ref),
+        (gain_hbm, gain_ref),
+    )
     loads = [
         pltpu.make_async_copy(src, dst, in_sem.at[i]) for i, (src, dst) in enumerate(pairs)
     ]
@@ -79,9 +77,8 @@
     pieces = BLK // width
     pad = [jnp.zeros((rows - nblk, width), F32)] if rows > nblk else []
     loads[0].wait()
-    for b in range(nblk):
-        loads[1 + b].wait()
-        loads[1 + nblk + b].wait()
+    loads[1].wait()
+    loads[2].wait()
     x = jnp.concatenate(
         sum(
             (
@@ -193,8 +190,14 @@
         def _():
             hop(0, d).start()
 
-    loads[2 * nblk + 1].wait()
-    loads[2 * nblk + 3].wait()
+    loads[3].wait()
+    loads[5].wait()
+    before = jnp.zeros((1, width), F32)
+    for b in range(nblk):
+        flipped_ref[b] = jnp.transpose(state_ref[b])
+        scales_ref[b:b + 1, :] = jnp.exp(before)
+        before = before + a_row(b)
+    scales_ref[nblk:nblk + 1, :] = jnp.exp(before)
     gain_col = jnp.transpose(jnp.broadcast_to(gain_ref[...], (width, width)))
     diagonal = lax.broadcasted_iota(jnp.int32, (TILE, TILE), 0) <= lax.broadcasted_iota(
         jnp.int32, (TILE, TILE), 1
@@ -222,19 +225,17 @@
                 out_ref[:, span(b)] = part
             else:
                 out_ref[:, span(b, s0, rest)] += part
-    loads[2 * nblk + 2].wait()
+    loads[4].wait()
     for b in range(nblk):
         scaled_ref[:, span(b)] = lanes(gain_col, BLK) * flip(y_ref[span(b), :])
 
     entering = receive()
-    before = jnp.zeros((1, width), F32)
+    flipped = jnp.transpose(entering)
     if stat_ref.shape[0] > 2 * nblk:
         stat_ref[...] = jnp.zeros_like(stat_ref)
     for b in range(nblk):
-        held = state_ref[b] + jnp.exp(before) * entering
-        before = before + a_row(b)
-        held_ref[b] = held.astype(BF16)
-        carried = dot(jnp.transpose(held).astype(BF16), qt_ref[:, span(b)])
+        held = flipped_ref[b] + scales_ref[b:b + 1, :] * flipped
+        carried = dot(held.astype(BF16), qt_ref[:, span(b)])
         out = out_ref[:, span(b)] + jnp.exp(c_row(b)) * carried
         out_ref[:, span(b)] = out
         stat_ref[b:b + 1, :] = jnp.sum(out * out, axis=0, keepdims=True)
@@ -243,36 +244,54 @@
         )
 
     def share(d):
+        if n_head & (n_head - 1):
+            partner = lax.rem(head + d, n_head)
+        else:
+            partner = head
+            for bit in range(n_head.bit_length()):
+                if d >> bit & 1:
+                    partner = partner + (1 - 2 * lax.rem(head // (1 << bit), 2)) * (1 << bit)
         return pltpu.make_async_remote_copy(
             src_ref=stat_ref,
             dst_ref=stats_ref.at[d - 1],
-            send_sem=hsend_sem.at[d - 1],
-            recv_sem=hrecv_sem.at[d - 1],
-            device_id={"head": lax.rem(head + d, n_head)},
+            send_sem=hsend_sem.at[0],
+            recv_sem=hrecv_sem.at[0],
+            device_id={"head": partner},
             device_id_type=MESH,
         )
 
-    for d in range(1, n_head):
+    shares = pltpu.make_async_remote_copy(
+        src_ref=stats_ref,
+        dst_ref=stats_ref,
+        send_sem=hsend_sem.at[0],
+        recv_sem=hrecv_sem.at[0],
+        device_id={"head": lax.rem(head + 1, n_head)},
+        device_id_type=MESH,
+    )
+
+    for d in sorted(range(1, n_head), key=lambda d: -(d >> 1).bit_count()):
         share(d).start()
+    shares.wait_recv()
     total = stat_ref[...]
     for d in range(1, n_head):
-        share(d).wait_recv()
         total = total + stats_ref[d - 1]
     inv = lax.rsqrt(total[:nblk] / features + EPS)
     coef = inv * inv * inv * total[nblk:2 * nblk] / features
 
     rear = jnp.zeros((width, width), F32)
-    for b in reversed(range(nblk)):
+    for b in range(nblk):
         dout = (
             inv[b:b + 1] * scaled_ref[:, span(b)] - out_ref[:, span(b)] * coef[b:b + 1]
         ).astype(BF16)
         dout_ref[:, span(b)] = dout
-        rear_ref[b] = rear
-        rear = jnp.exp(a_row(b)) * rear + dot(queried_ref[:, span(b)], dout, 1, 1)
+        piece = dot(queried_ref[:, span(b)], dout, 1, 1)
+        rear_ref[b] = piece
+        rear = rear + scales_ref[b:b + 1, :] * piece
     rear_ref[nblk] = rear
     send_back(True)
 
     for b in range(nblk):
+        held_ref[b] = (state_ref[b] + scales_ref[b:b + 1, :] * entering).astype(BF16)
         grad_q = jnp.exp(c_row(b)) * dot(held_ref[b], dout_ref[:, span(b)])
         halves = [grad_q[:, i * TILE:(i + 1) * TILE] for i in range(tiles)]
         for i in range(tiles):
@@ -292,6 +311,11 @@
         if b == min(1, nblk - 1):
             send_back(False)
 
+    rear = jnp.zeros((width, width), F32)
+    for b in reversed(range(nblk)):
+        piece = rear_ref[b]
+        rear_ref[b] = rear
+        rear = jnp.exp(a_row(b)) * rear + piece
     leaving = receive_back()
     after = jnp.zeros((1, width), F32)
     for b in reversed(range(nblk)):
@@ -300,8 +324,7 @@
 
     finish(0)
     finish(1)
-    for d in range(1, n_head):
-        share(d).wait_send()
+    shares.wait_send()
 
 
 def closing(
@@ -375,11 +398,13 @@
             pltpu.VMEM((n_seq - 1, width, width), F32),
             pltpu.VMEM((n_seq - 1, width, width), F32),
             pltpu.VMEM((n_seq, width), F32),
+            pltpu.VMEM((nblk, width, width), F32),
+            pltpu.VMEM((nblk + 1, width), F32),
             pltpu.VMEM((srows, BLK), F32),
             pltpu.VMEM((n_head - 1, srows, BLK), F32),
-            dma((2 * nblk + 4,)),
+            dma((6,)),
             dma((2, n_seq - 1)), dma((2, n_seq - 1)),
-            dma((n_head - 1,)), dma((n_head - 1,)),
+            dma((1,)), dma((1,)),
         ],
         compiler_params=pltpu.CompilerParams(
             collective_id=0, has_side_effects=True, vmem_limit_bytes=40 << 20

time: 24.3 us -> 24.1 us (level)
  no operation moved by 1% of the time
where the time goes in v4:
time: 24.1 us; the launch traced here: 23.9 us
  Pallas kernels  23.2 us (96%)
  between operations  0.64 us (3%)
    pallas_call x1, Pallas kernels, shards(): pl.pallas_call(functools.partial(kernel, n_seq, n_head, features), out_sh...  21.9 us
    pallas_call x1, Pallas kernels, shards(): pl.pallas_call(closing, out_shape=(shape, shape, shape), in_specs=[vmem]...  1.27 us

profile of v4, /device:TPU:0, one launch (start us, length us, event | category | flops | bytes accessed | tf_op | source)
XLA Modules:
  0.0 23.9 jit_solution(15897207024362332254)
XLA Ops:
  0.6 21.9 %shard_map.85 = (bf16[2048,128]{1,0:T(8,128)(2,1)S(1)}, bf16[2048,128]{1,0:T(8,128)(2,1)S(1)}, bf16[2048,128]{1,0:T(8,128)(2,1)S(1)}, f32[2048,128]{1,0:T(8,128)...) custom-call(bf16[2048,128]{1,0:T(8,128)(2,1)} %q_hbm.1, ...), custom_call_target="tpu_custom_call" | custom-call | tf_op jit(solution)/shard_map/pallas_call | solution.py:377
  22.6 1.3 %shard_map.86 = (bf16[2048,128]{1,0:T(8,128)(2,1)}, bf16[2048,128]{1,0:T(8,128)(2,1)}, bf16[2048,128]{1,0:T(8,128)(2,1)}) custom-call(bf16[2048,128]{1,0:T(8,128)(2,1)S(1)} %get-tuple-element.10.oq_ref, bf16[2048,128]{1,0:T(8,128)(2,1)S(1)} %get-tuple-element.11.k_ref, bf16[2048,128]{1,0:T(8,128)(2,1)S(1)} %get-tuple-element.12.v_ref, ...), custom_call_target="tpu_custom_call" | custom-call | tf_op jit(solution)/shard_map/pallas_call | solution.py:413

commit v5 on v4

--- a/solution.py
+++ b/solution.py
@@ -37,7 +37,7 @@
     c_ref, a_ref, col_ref, inner_ref, mix_ref, out_ref, dout_ref,
     state_ref, rear_ref, held_ref, edge_ref,
     tx_ref, rx_ref, back_ref, rear_rx_ref, scale_ref, flipped_ref, scales_ref, stat_ref, stats_ref,
-    in_sem, send_sem, recv_sem, hsend_sem, hrecv_sem,
+    in_sem, know_sem, send_sem, recv_sem, hsend_sem, hrecv_sem,
 ):
     seq = lax.axis_index("seq")
     head = lax.axis_index("head")
@@ -46,10 +46,15 @@
     tiles = BLK // TILE
 
     barrier = pltpu.get_barrier_semaphore()
-    for d in range(1, n_seq):
-        pl.semaphore_signal(
-            barrier, inc=1, device_id={"seq": lax.rem(seq + d, n_seq)}, device_id_type=MESH
-        )
+    for step in (-1, 1):
+        @pl.when((seq + step >= 0) & (seq + step < n_seq))
+        def _():
+            pl.semaphore_signal(
+                barrier,
+                inc=1,
+                device_id={"seq": lax.rem(seq + step + n_seq, n_seq)},
+                device_id_type=MESH,
+            )
     for d in range(1, n_head):
         pl.semaphore_signal(
             barrier, inc=1, device_id={"head": lax.rem(head + d, n_head)}, device_id_type=MESH
@@ -127,7 +132,26 @@
     tx_ref[:width, :] = state
     tx_ref[width:, :] = jnp.broadcast_to(own, (8, width))
 
-    pl.semaphore_wait(barrier, n_seq - 1 + n_head - 1)
+    inner = (seq > 0) & (seq < n_seq - 1)
+
+    @pl.when(inner)
+    def _():
+        pl.semaphore_wait(barrier, n_head + 1)
+
+    @pl.when(jnp.logical_not(inner))
+    def _():
+        pl.semaphore_wait(barrier, n_head if n_seq > 1 else n_head - 1)
+
+    def tell(d):
+        pl.semaphore_signal(
+            know_sem.at[d],
+            inc=1,
+            device_id={"seq": lax.rem(seq - 1 + n_seq, n_seq)},
+            device_id_type=MESH,
+        )
+
+    if n_seq > 2:
+        pl.when(inner)(lambda: tell(2))
 
     def hop(way, d):
         if way == 0:
@@ -185,10 +209,17 @@
             def _():
                 hop(way, d).wait_send()
 
-    for d in range(1, n_seq):
+    def send(d):
         @pl.when(reaches(0, d))
         def _():
+            if d > 1:
+                pl.semaphore_wait(know_sem.at[d], 1)
+            if d > 1 and d + 1 < n_seq:
+                pl.when(seq > 0)(lambda: tell(d + 1))
             hop(0, d).start()
+
+    if n_seq > 1:
+        send(1)
 
     loads[3].wait()
     loads[5].wait()
@@ -225,6 +256,9 @@
                 out_ref[:, span(b)] = part
             else:
                 out_ref[:, span(b, s0, rest)] += part
+        for d in range(2 + b, 3 + b if b < nblk - 1 else n_seq):
+            if d < n_seq:
+                send(d)
     loads[4].wait()
     for b in range(nblk):
         scaled_ref[:, span(b)] = lanes(gain_col, BLK) * flip(y_ref[span(b), :])
@@ -403,6 +437,7 @@
             pltpu.VMEM((srows, BLK), F32),
             pltpu.VMEM((n_head - 1, srows, BLK), F32),
             dma((6,)),
+            pltpu.SemaphoreType.REGULAR((n_seq,)),
             dma((2, n_seq - 1)), dma((2, n_seq - 1)),
             dma((1,)), dma((1,)),
         ],

time: 24.1 us -> 23.8 us (0.988)
  Pallas kernels: 23.2 us -> 22.9 us
    pallas_call x1, Pallas kernels: 21.9 us -> 21.7 us  [shards(): pl.pallas_call(functools.partial(kernel, n_seq, n_head, features), out_sh...]
where the time goes in v5:
time: 23.8 us; the launch traced here: 23.6 us
  Pallas kernels  22.9 us (96%)
  between operations  0.64 us (3%)
    pallas_call x1, Pallas kernels, shards(): pl.pallas_call(functools.partial(kernel, n_seq, n_head, features), out_sh...  21.7 us
    pallas_call x1, Pallas kernels, shards(): pl.pallas_call(closing, out_shape=(shape, shape, shape), in_specs=[vmem]...  1.26 us

profile of v5, /device:TPU:0, one launch (start us, length us, event | category | flops | bytes accessed | tf_op | source)
XLA Modules:
  0.0 23.6 jit_solution(11775417773770071873)
XLA Ops:
  0.6 21.7 %shard_map.85 = (bf16[2048,128]{1,0:T(8,128)(2,1)S(1)}, bf16[2048,128]{1,0:T(8,128)(2,1)S(1)}, bf16[2048,128]{1,0:T(8,128)(2,1)S(1)}, f32[2048,128]{1,0:T(8,128)...) custom-call(bf16[2048,128]{1,0:T(8,128)(2,1)} %q_hbm.1, ...), custom_call_target="tpu_custom_call" | custom-call | tf_op jit(solution)/shard_map/pallas_call | solution.py:411
  22.3 1.3 %shard_map.86 = (bf16[2048,128]{1,0:T(8,128)(2,1)}, bf16[2048,128]{1,0:T(8,128)(2,1)}, bf16[2048,128]{1,0:T(8,128)(2,1)}) custom-call(bf16[2048,128]{1,0:T(8,128)(2,1)S(1)} %get-tuple-element.10.oq_ref, bf16[2048,128]{1,0:T(8,128)(2,1)S(1)} %get-tuple-element.11.k_ref, bf16[2048,128]{1,0:T(8,128)(2,1)S(1)} %get-tuple-element.12.v_ref, ...), custom_call_target="tpu_custom_call" | custom-call | tf_op jit(solution)/shard_map/pallas_call | solution.py:448

commit v6 on v5

--- a/solution.py
+++ b/solution.py
@@ -323,6 +323,7 @@
         rear = rear + scales_ref[b:b + 1, :] * piece
     rear_ref[nblk] = rear
     send_back(True)
+    pl.when(seq < n_seq - 1)(lambda: send_back(False))
 
     for b in range(nblk):
         held_ref[b] = (state_ref[b] + scales_ref[b:b + 1, :] * entering).astype(BF16)
@@ -342,8 +343,8 @@
         for i in range(tiles):
             oq_ref[span(b, i * TILE, TILE), :] = jnp.transpose(halves[i]).astype(BF16)
         end_ref[span(b), :] = jnp.exp(a_row(b) - col_ref[span(b), :])
-        if b == min(1, nblk - 1):
-            send_back(False)
+        if b == min(2, nblk - 1):
+            pl.when(seq == n_seq - 1)(lambda: send_back(False))
 
     rear = jnp.zeros((width, width), F32)
     for b in reversed(range(nblk)):

time: 23.8 us -> 23.7 us (level)
  no operation moved by 1% of the time
where the time goes in v6:
time: 23.7 us; the launch traced here: 23.4 us
  Pallas kernels  22.8 us (96%)
  between operations  0.64 us (3%)
    pallas_call x1, Pallas kernels, shards(): pl.pallas_call(functools.partial(kernel, n_seq, n_head, features), out_sh...  21.5 us
    pallas_call x1, Pallas kernels, shards(): pl.pallas_call(closing, out_shape=(shape, shape, shape), in_specs=[vmem]...  1.26 us

profile of v6, /device:TPU:0, one launch (start us, length us, event | category | flops | bytes accessed | tf_op | source)
XLA Modules:
  0.0 23.4 jit_solution(14862236637051680163)
XLA Ops:
  0.6 21.5 %shard_map.85 = (bf16[2048,128]{1,0:T(8,128)(2,1)S(1)}, bf16[2048,128]{1,0:T(8,128)(2,1)S(1)}, bf16[2048,128]{1,0:T(8,128)(2,1)S(1)}, f32[2048,128]{1,0:T(8,128)...) custom-call(bf16[2048,128]{1,0:T(8,128)(2,1)} %q_hbm.1, ...), custom_call_target="tpu_custom_call" | custom-call | tf_op jit(solution)/shard_map/pallas_call | solution.py:412
  22.2 1.3 %shard_map.86 = (bf16[2048,128]{1,0:T(8,128)(2,1)}, bf16[2048,128]{1,0:T(8,128)(2,1)}, bf16[2048,128]{1,0:T(8,128)(2,1)}) custom-call(bf16[2048,128]{1,0:T(8,128)(2,1)S(1)} %get-tuple-element.10.oq_ref, bf16[2048,128]{1,0:T(8,128)(2,1)S(1)} %get-tuple-element.11.k_ref, bf16[2048,128]{1,0:T(8,128)(2,1)S(1)} %get-tuple-element.12.v_ref, ...), custom_call_target="tpu_custom_call" | custom-call | tf_op jit(solution)/shard_map/pallas_call | solution.py:449

commit v7 on v6

--- a/solution.py
+++ b/solution.py
@@ -378,12 +378,10 @@
     stores = []
     for b in range(nblk):
         ending = end_ref[span(b), :]
-        ok_ref[span(b), :] = (
-            gk_ref[span(b), :] + ending * dot(v_ref[span(b), :], kept_ref[b], 1, 1)
-        ).astype(BF16)
-        ov_ref[span(b), :] = (
-            gv_ref[span(b), :] + ending * dot(k_ref[span(b), :], kept_ref[b])
-        ).astype(BF16)
+        by_value = dot(v_ref[span(b), :], kept_ref[b], 1, 1)
+        by_key = dot(k_ref[span(b), :], kept_ref[b])
+        ok_ref[span(b), :] = (gk_ref[span(b), :] + ending * by_value).astype(BF16)
+        ov_ref[span(b), :] = (gv_ref[span(b), :] + ending * by_key).astype(BF16)
         for i, (src, dst) in enumerate(((ok_ref, gk_hbm), (ov_ref, gv_hbm))):
             store = pltpu.make_async_copy(
                 src.at[span(b), :], dst.at[span(b), :], out_sem.at[2 * b + i]

time: 23.7 us -> 23.7 us (level)
  no operation moved by 1% of the time
where the time goes in v7:
time: 23.7 us; the launch traced here: 23.4 us
  Pallas kernels  22.8 us (96%)
  between operations  0.64 us (3%)
    pallas_call x1, Pallas kernels, shards(): pl.pallas_call(functools.partial(kernel, n_seq, n_head, features), out_sh...  21.5 us
    pallas_call x1, Pallas kernels, shards(): pl.pallas_call(closing, out_shape=(shape, shape, shape), in_specs=[vmem]...  1.26 us

profile of v7, /device:TPU:0, one launch (start us, length us, event | category | flops | bytes accessed | tf_op | source)
XLA Modules:
  0.0 23.4 jit_solution(15864327368213623411)
XLA Ops:
  0.6 21.5 %shard_map.85 = (bf16[2048,128]{1,0:T(8,128)(2,1)S(1)}, bf16[2048,128]{1,0:T(8,128)(2,1)S(1)}, bf16[2048,128]{1,0:T(8,128)(2,1)S(1)}, f32[2048,128]{1,0:T(8,128)...) custom-call(bf16[2048,128]{1,0:T(8,128)(2,1)} %q_hbm.1, ...), custom_call_target="tpu_custom_call" | custom-call | tf_op jit(solution)/shard_map/pallas_call | solution.py:410
  22.2 1.3 %shard_map.86 = (bf16[2048,128]{1,0:T(8,128)(2,1)}, bf16[2048,128]{1,0:T(8,128)(2,1)}, bf16[2048,128]{1,0:T(8,128)(2,1)}) custom-call(bf16[2048,128]{1,0:T(8,128)(2,1)S(1)} %get-tuple-element.10.oq_ref, bf16[2048,128]{1,0:T(8,128)(2,1)S(1)} %get-tuple-element.11.k_ref, bf16[2048,128]{1,0:T(8,128)(2,1)S(1)} %get-tuple-element.12.v_ref, ...), custom_call_target="tpu_custom_call" | custom-call | tf_op jit(solution)/shard_map/pallas_call | solution.py:447
